TPU v7x, 256 devices: a whole 4x4x8 slice. The times are simulated.
256 devices in a mesh: dp: 128 (over y, x_hi, z, core), mp: 2 (over x_lo).
Axes of the slice: x: 4 (x_hi: 2, x_lo: 2; x = x_hi * 2 + x_lo), y: 4, z: 8, core: 2. Of those that a mesh axis runs over, the one named last changes fastest.
Arguments:
- dino_tokens: bfloat16 [65536, 1024], P('dp', 'mp'), may hold values from -6 to 6
- siglip_tokens: bfloat16 [65536, 1152], P('dp', 'mp'), may hold values from -6 to 6
- dino_norm_one: float32 [1024], replicated, may hold values from 0.25 to 1.75
- dino_qkv: bfloat16 [1024, 3, 1024], P('dp', None, 'mp'), may hold values from -6.05625 to 6.05625
- dino_out: bfloat16 [1024, 1024], P('mp', 'dp'), may hold values from -0.1875 to 0.1875
- dino_norm_two: float32 [1024], replicated, may hold values from 0.25 to 1.75
- dino_up: bfloat16 [1024, 4096], P('dp', 'mp'), may hold values from -0.1875 to 0.1875
- dino_down: bfloat16 [4096, 1024], P('mp', 'dp'), may hold values from -0.09375 to 0.09375
- siglip_norm_one: float32 [1152], replicated, may hold values from 0.25 to 1.75
- siglip_qkv: bfloat16 [1152, 3, 1152], P('dp', None, 'mp'), may hold values from -5.709887 to 5.709887
- siglip_out: bfloat16 [1152, 1152], P('mp', 'dp'), may hold values from -0.1875 to 0.1875
- siglip_norm_two: float32 [1152], replicated, may hold values from 0.25 to 1.75
- siglip_up: bfloat16 [1152, 4304], P('dp', 'mp'), may hold values from -0.1875 to 0.1875
- siglip_down: bfloat16 [4304, 1152], P('mp', 'dp'), may hold values from -0.09375 to 0.09375
Outputs:
- dino_result: bfloat16 [65536, 1024], P('dp', 'mp')
- siglip_result: bfloat16 [65536, 1152], P('dp', 'mp')
All inputs are finite; a program needn't handle non-finite values.
Results may differ from a plain program's by a relative error of at most 0.012.
Values may be sent and summed in bfloat16 or wider, within the bound.
A program may use at most 128 MiB of HBM per device.

v0:
```python
import math
import jax
import jax.numpy as jnp
from jax import lax
from jax.sharding import PartitionSpec as P

HEADS = 16
PATCHES = 256
EPS = 1e-06


def from_everyone(shard, axis):
    size = lax.axis_size(axis)
    return lax.all_to_all(
        jnp.broadcast_to(shard[None], (size, *shard.shape)), axis, 0, 0, tiled=True
    )


def laid_out(pieces, dim):
    shape = list(pieces.shape[1:])
    shape[dim] *= pieces.shape[0]
    return jnp.moveaxis(pieces, 0, dim).reshape(shape)


def gathered_copies(shard, axis, dim):
    pieces = from_everyone(shard, axis)
    return laid_out(pieces, dim)


def split_up(shard, dim, size):
    shape = shard.shape
    pieces = shard.reshape(*shape[:dim], size, shape[dim] // size, *shape[dim + 1 :])
    return jnp.moveaxis(pieces, dim, 0)


def sum_at_owner(shard, axis, dim):
    pieces = split_up(shard, dim, lax.axis_size(axis))
    arrived = lax.all_to_all(pieces, axis, split_axis=0, concat_axis=0, tiled=True)
    return arrived.astype(jnp.float32).sum(axis=0)


def layer_norm(values, gain):
    values = values.astype(jnp.float32)
    center = values - jnp.mean(values, axis=-1, keepdims=True)
    spread = jnp.mean(center * center, axis=-1, keepdims=True)
    return (center * lax.rsqrt(spread + EPS) * gain).astype(jnp.bfloat16)


def encoder(tokens, norm_one, qkv_weight, out_weight, norm_two, up_weight, down_weight, approx):
    rows, local_width = tokens.shape
    whole = gathered_copies(tokens, "mp", 1)
    width = whole.shape[1]
    head_size = width // HEADS
    local_heads = qkv_weight.shape[2] // head_size
    scale = 1.0 / math.sqrt(head_size)
    normed = layer_norm(whole, norm_one)

    def fold_rows(source, piece):
        count = piece.shape[0]
        return jnp.dot(source, piece.reshape(count, -1), preferred_element_type=jnp.float32)

    qkv = fold_rows(normed, lax.all_gather(qkv_weight, "dp", axis=0, tiled=True))
    qkv = qkv.astype(jnp.bfloat16).reshape(rows // PATCHES, PATCHES, 3, local_heads, head_size)
    query = qkv[:, :, 0]
    keys = qkv[:, :, 1]
    values = qkv[:, :, 2]
    scores = jnp.einsum("fqhd,fkhd->fhqk", query, keys, preferred_element_type=jnp.float32) * scale
    top = jnp.max(scores, axis=-1, keepdims=True)
    expo = jnp.exp(scores - top)
    probs = (expo / jnp.sum(expo, axis=-1, keepdims=True)).astype(jnp.bfloat16)
    context = jnp.einsum("fhqk,fkhd->fqhd", probs, values, preferred_element_type=jnp.float32)
    context = context.astype(jnp.bfloat16).reshape(rows, local_heads * head_size)
    partial_attn = jnp.dot(
        context,
        lax.all_gather(out_weight, "dp", axis=1, tiled=True),
        preferred_element_type=jnp.float32,
    )
    share = sum_at_owner(partial_attn.astype(jnp.bfloat16), "mp", 1)
    middle = (tokens.astype(jnp.float32) + share).astype(jnp.bfloat16)
    middle_whole = gathered_copies(middle, "mp", 1)
    second = layer_norm(middle_whole, norm_two)
    raised = fold_rows(second, lax.all_gather(up_weight, "dp", axis=0, tiled=True))
    hidden = jax.nn.gelu(raised, approximate=approx).astype(jnp.bfloat16)
    partial_mlp = jnp.dot(
        hidden,
        lax.all_gather(down_weight, "dp", axis=1, tiled=True),
        preferred_element_type=jnp.float32,
    )
    mlp_part = sum_at_owner(partial_mlp.astype(jnp.bfloat16), "mp", 1)
    return (middle.astype(jnp.float32) + mlp_part).astype(jnp.bfloat16)


def local(
    dino_tokens,
    siglip_tokens,
    dino_norm_one,
    dino_qkv,
    dino_out,
    dino_norm_two,
    dino_up,
    dino_down,
    siglip_norm_one,
    siglip_qkv,
    siglip_out,
    siglip_norm_two,
    siglip_up,
    siglip_down,
):
    dino_result = encoder(
        dino_tokens, dino_norm_one, dino_qkv, dino_out, dino_norm_two, dino_up, dino_down, False
    )
    siglip_result = encoder(
        siglip_tokens,
        siglip_norm_one,
        siglip_qkv,
        siglip_out,
        siglip_norm_two,
        siglip_up,
        siglip_down,
        True,
    )
    return (dino_result, siglip_result)


def solution(mesh):
    in_specs = (
        P("dp", "mp"),
        P("dp", "mp"),
        P(),
        P("dp", None, "mp"),
        P("mp", "dp"),
        P(),
        P("dp", "mp"),
        P("mp", "dp"),
        P(),
        P("dp", None, "mp"),
        P("mp", "dp"),
        P(),
        P("dp", "mp"),
        P("mp", "dp"),
    )
    out_specs = (P("dp", "mp"), P("dp", "mp"))
    return jax.shard_map(local, mesh=mesh, in_specs=in_specs, out_specs=out_specs, check_vma=False)
```

profile of v0, /device:TPU:1, one launch (start us, length us, event | category | flops | bytes accessed | tf_op | source)
XLA Modules:
  0.0 1024.6 jit_solution(13799758242859776503)
XLA Ops:
  11.9 1.3 copy.43
  14.2 3.6 all-to-all-start
  17.8 11.6 %all-to-all-done = bf16[2,512,512]{1,2,0:T(8,128)(2,1)S(1)} async-done(((bf16[2,512,512]{1,2,0:T(8,128)(2,1)}), bf16[2,512,512]{1,2,0:T(8,128)(2,1)S(1)}, u32[]{:S(2)}, u32[]{:S(2)}) %all-to-all-start) | async-done | bytes 1048608 | tf_op jit(solution)/shard_map/all_to_all | solution.py:14
  30.6 3.6 all-to-all-start.4
  34.7 1.3 fusion.43
  36.1 90.8 %all-gather.12.cloned.1.call-done = bf16[1024,3,512]{2,0,1:T(8,128)(2,1)} async-done(((bf16[8,3,512]{2,0,1:T(8,128)(2,1)}), bf16[1024,3,512]{2,0,1:T(8,128)(2,1)}) %all-gather.12.cloned.1.call-update) | async-done | bytes 3145744 | tf_op jit(solution)/shard_map/all_gather | solution.py:62
  126.8 4.7 copy.44
  131.5 4.1 convolution_convert_fusion.2
  135.6 3.2 reshape.172
  138.7 3.1 fusion.101
  141.8 2.5 copy.67
  144.3 1.4 copy.68
  146.3 2.0 fusion.61
  148.3 3.2 fusion.103
  152.7 78.1 %all-gather.14.cloned.1.call-done = bf16[512,1024]{0,1:T(8,128)(2,1)} async-done(((bf16[512,8]{0,1:T(8,128)(2,1)}), bf16[512,1024]{0,1:T(8,128)(2,1)}) %all-gather.14.cloned.1.call-update) | async-done | bytes 1048592 | tf_op jit(solution)/shard_map/all_gather | solution.py:75
  230.8 2.0 convolution_convert_fusion.4
  233.9 3.6 all-to-all-start.1
  238.5 12.6 %all-to-all-done.1 = bf16[2,512,512]{2,1,0:T(8,128)(2,1)S(1)} async-done(((bf16[2,512,512]{2,1,0:T(8,128)(2,1)}), bf16[2,512,512]{2,1,0:T(8,128)(2,1)S(1)}, u32[]{:S(2)}, u32[]{:S(2)}) %all-to-all-start.1) | async-done | bytes 1048608 | tf_op jit(solution)/shard_map/all_to_all | solution.py:38
  252.8 4.0 all-to-all-start.2
  257.2 1.4 fusion.32
  258.6 91.0 %all-gather.22.cloned.1.call-done = bf16[128,9,576]{2,1,0:T(8,128)(2,1)} async-done(((bf16[1,9,576]{2,1,0:T(8,128)(2,1)}), bf16[128,9,576]{2,1,0:T(8,128)(2,1)}) %all-gather.22.cloned.1.call-update) | async-done | bytes 1327120 | tf_op jit(solution)/shard_map/all_gather | solution.py:75
  349.6 4.1 reshape.167
  353.9 118.7 %all-gather.20.cloned.1.call-done = bf16[1152,3,576]{2,1,0:T(4,128)(2,1)} async-done(((bf16[9,3,576]{2,1,0:T(4,128)(2,1)}), bf16[1152,3,576]{2,1,0:T(4,128)(2,1)}) %all-gather.20.cloned.1.call-update) | async-done | bytes 3981328 | tf_op jit(solution)/shard_map/all_gather | solution.py:62
  472.6 11.3 %copy.54 = bf16[1152,3,576]{0,2,1:T(8,128)(2,1)} copy(bf16[1152,3,576]{2,1,0:T(4,128)(2,1)} %all-gather.20.cloned.1.call-done) | data formatting | bytes 7962624 | tf_op jit(solution)/shard_map/all_gather | solution.py:62
  484.0 5.8 convolution_convert_fusion
  489.8 4.8 reshape.160
  494.6 2.6 fusion.102
  498.0 3.2 fusion.104
  503.9 1.5 copy.60
  505.3 3.7 all-to-all-start.5
  509.4 1.3 fusion.46
  510.7 13.2 %all-to-all-done.5 = bf16[2,512,576]{1,2,0:T(8,128)(2,1)S(1)} async-done(((bf16[2,512,576]{1,2,0:T(8,128)(2,1)}), bf16[2,512,576]{1,2,0:T(8,128)(2,1)S(1)}, u32[]{:S(2)}, u32[]{:S(2)}) %all-to-all-start.5) | async-done | bytes 1179680 | tf_op jit(solution)/shard_map/all_to_all | solution.py:38
  525.5 3.8 all-to-all-start.6
  529.3 63.4 %all-gather.16.cloned.1.call-done = bf16[1024,2048]{1,0:T(8,128)(2,1)} async-done(((bf16[8,2048]{1,0:T(8,128)(2,1)}), bf16[1024,2048]{1,0:T(8,128)(2,1)}) %all-gather.16.cloned.1.call-update) | async-done | bytes 4194320 | tf_op jit(solution)/shard_map/all_gather | solution.py:82
  592.7 120.0 %all-gather.18.cloned.1.call-done = bf16[2048,1024]{0,1:T(8,128)(2,1)} async-done(((bf16[2048,8]{0,1:T(8,128)(2,1)}), bf16[2048,1024]{0,1:T(8,128)(2,1)}) %all-gather.18.cloned.1.call-update) | async-done | bytes 4194320 | tf_op jit(solution)/shard_map/all_gather | solution.py:86
  712.7 17.9 %fusion.53 = bf16[512,1024]{1,0:T(8,128)(2,1)} fusion(bf16[2048,1024]{0,1:T(8,128)(2,1)} %all-gather.18.cloned.1.call-done, bf16[512,1024]{0,1:T(8,128)(2,1)} %fusion.46, bf16[1024,2048]{1,0:T(8,128)(2,1)} %all-gather.16.cloned.1.call-done), kind=kOutput, calls=%fused_computation.79 | convolution fusion | flops 4363649024 | bytes 10485760 | tf_op jit(solution)/shard_map/dot_general | solution.py:84
  730.7 2.3 copy.84
  733.0 4.5 all-to-all-start.3
  738.1 1.4 fusion.35
  739.5 103.9 %all-gather.24.cloned.1.call-done = bf16[128,9,2152]{2,1,0:T(8,128)(2,1)} async-done(((bf16[1,9,2152]{2,1,0:T(8,128)(2,1)}), bf16[128,9,2152]{2,1,0:T(8,128)(2,1)}) %all-gather.24.cloned.1.call-update) | async-done | bytes 4958224 | tf_op jit(solution)/shard_map/all_gather | solution.py:82
  843.4 9.1 reshape.169
  852.5 121.5 %all-gather.26.cloned.1.call-done = bf16[128,9,2152]{2,1,0:T(8,128)(2,1)} async-done(((bf16[1,9,2152]{2,1,0:T(8,128)(2,1)}), bf16[128,9,2152]{2,1,0:T(8,128)(2,1)}) %all-gather.26.cloned.1.call-update) | async-done | bytes 4958224 | tf_op jit(solution)/shard_map/all_gather | solution.py:86
  974.1 9.1 reshape.171
  983.2 12.2 %convolution_convert_fusion.3 = bf16[512,1152]{1,0:T(8,128)(2,1)} fusion(bf16[1152,2152]{1,0:T(8,128)(2,1)} %reshape.171, bf16[512,1152]{0,1:T(8,128)(2,1)S(1)} %copy-done.5, bf16[1152,2152]{1,0:T(8,128)(2,1)} %reshape.169), kind=kOutput, calls=%fused_computation.41 | convolution fusion | flops 5087711232 | bytes 12275712 | tf_op jit(solution)/shard_map/dot_general | solution.py:84
  995.4 2.4 copy.61
  997.8 3.6 all-to-all-start.7
  1001.4 1.5 convert_reduce_fusion.4
  1003.9 12.4 %all-to-all-done.7 = bf16[2,512,576]{1,2,0:T(8,128)(2,1)S(1)} async-done(((bf16[2,512,576]{1,2,0:T(8,128)(2,1)}), bf16[2,512,576]{1,2,0:T(8,128)(2,1)S(1)}, u32[]{:S(2)}, u32[]{:S(2)}) %all-to-all-start.7) | async-done | bytes 1179680 | tf_op jit(solution)/shard_map/all_to_all | solution.py:38
  (80 shorter events, 21.6 us)
Async XLA Ops:
  7.2 10.7 %copy-start.9 = (f32[1024]{0:T(1024)S(1)}, f32[1024]{0:T(1024)}, u32[]{:S(2)}) copy-start(f32[1024]{0:T(1024)} %param.16) | copy-start | bytes 12292
  7.2 22.3 %copy-start = (bf16[512,576]{0,1:T(8,128)(2,1)S(1)}, bf16[512,576]{0,1:T(8,128)(2,1)}, u32[]{:S(2)}) copy-start(bf16[512,576]{0,1:T(8,128)(2,1)} %param.15) | copy-start | bytes 1769476
  7.2 119.6 %all-gather.12.cloned.1.call-start = ((), (), s32[]{:S(2)}) async-start(), calls=%async_computation.8 | async-start | bytes 3170304 | tf_op jit(solution)/shard_map/all_gather | solution.py:62
  7.9 222.9 %all-gather.14.cloned.1.call-start = ((), (), s32[]{:S(2)}) async-start(), calls=%async_computation.9 | async-start | bytes 1056768 | tf_op jit(solution)/shard_map/all_gather | solution.py:75
  8.7 340.9 %all-gather.22.cloned.1.call-start = ((), (), s32[]{:S(2)}) async-start(), calls=%async_computation.13 | async-start | bytes 2641920 | tf_op jit(solution)/shard_map/all_gather | solution.py:75
  9.4 463.2 %all-gather.20.cloned.1.call-start = ((), (), s32[]{:S(2)}) async-start(), calls=%async_computation.12 | async-start | bytes 5944320 | tf_op jit(solution)/shard_map/all_gather | solution.py:62
  10.0 582.7 %all-gather.16.cloned.1.call-start = ((), (), s32[]{:S(2)}) async-start(), calls=%async_computation.10 | async-start | bytes 4227072 | tf_op jit(solution)/shard_map/all_gather | solution.py:82
  10.6 702.2 %all-gather.18.cloned.1.call-start = ((), (), s32[]{:S(2)}) async-start(), calls=%async_computation.11 | async-start | bytes 4227072 | tf_op jit(solution)/shard_map/all_gather | solution.py:86
  11.1 832.3 %all-gather.24.cloned.1.call-start = ((), (), s32[]{:S(2)}) async-start(), calls=%async_computation.14 | async-start | bytes 8982528 | tf_op jit(solution)/shard_map/all_gather | solution.py:82
  14.2 15.2 %all-to-all-start = ((bf16[2,512,512]{1,2,0:T(8,128)(2,1)}), bf16[2,512,512]{1,2,0:T(8,128)(2,1)S(1)}, u32[]{:S(2)}, u32[]{:S(2)}) async-start(bf16[2,512,512]{1,2,0:T(8,128)(2,1)} %broadcast_in_dim.8), calls=%async_computation | async-start | bytes 2097152 | tf_op jit(solution)/shard_map/all_to_all | solution.py:14
  30.6 203.3 %all-to-all-start.4 = ((bf16[2,512,576]{1,2,0:T(8,128)(2,1)}), bf16[2,512,576]{1,2,0:T(8,128)(2,1)S(1)}, u32[]{:S(2)}, u32[]{:S(2)}) async-start(bf16[2,512,576]{1,2,0:T(8,128)(2,1)} %broadcast_in_dim.10), calls=%async_computation.4 | async-start | bytes 2359296 | tf_op jit(solution)/shard_map/all_to_all | solution.py:14
  152.6 85.7 %copy-start.7 = (f32[1152]{0:T(1024)S(1)}, f32[1152]{0:T(1024)}, u32[]{:S(2)}) copy-start(f32[1152]{0:T(1024)} %param.22) | copy-start | bytes 13828
  232.8 18.5 %copy-start.2 = (bf16[512,512]{1,0:T(8,128)(2,1)S(1)}, bf16[512,512]{1,0:T(8,128)(2,1)}, u32[]{:S(2)}) copy-start(bf16[512,512]{1,0:T(8,128)(2,1)} %param.14) | copy-start | bytes 1572868
  233.9 17.2 %all-to-all-start.1 = ((bf16[2,512,512]{2,1,0:T(8,128)(2,1)}), bf16[2,512,512]{2,1,0:T(8,128)(2,1)S(1)}, u32[]{:S(2)}, u32[]{:S(2)}) async-start(bf16[2,512,512]{2,1,0:T(8,128)(2,1)} %bitcast.102), calls=%async_computation.1 | async-start | bytes 2097152 | tf_op jit(solution)/shard_map/all_to_all | solution.py:38
  237.5 736.6 %all-gather.26.cloned.1.call-start = ((), (), s32[]{:S(2)}) async-start(), calls=%async_computation.15 | async-start | bytes 8982528 | tf_op jit(solution)/shard_map/all_gather | solution.py:86
  252.8 100.9 %all-to-all-start.2 = ((bf16[2,512,512]{1,2,0:T(8,128)(2,1)}), bf16[2,512,512]{1,2,0:T(8,128)(2,1)S(1)}, u32[]{:S(2)}, u32[]{:S(2)}) async-start(bf16[2,512,512]{1,2,0:T(8,128)(2,1)} %broadcast_in_dim.9), calls=%async_computation.2 | async-start | bytes 2097152 | tf_op jit(solution)/shard_map/all_to_all | solution.py:14
  353.9 130.0 %copy-start.4 = (bf16[2,512,576]{1,2,0:T(8,128)(2,1)S(1)}, bf16[2,512,576]{1,2,0:T(8,128)(2,1)}, u32[]{:S(2)}) copy-start(bf16[2,512,576]{1,2,0:T(8,128)(2,1)} %fusion.32) | copy-start | bytes 3538948
  501.2 1.4 copy-start.3
  502.6 6.8 copy-start.8
  505.3 18.8 %copy-start.1 = (bf16[512,576]{0,1:T(8,128)(2,1)S(1)}, bf16[512,576]{0,1:T(8,128)(2,1)}, u32[]{:S(2)}) copy-start(bf16[512,576]{0,1:T(8,128)(2,1)} %param.15) | copy-start | bytes 1769476
  505.3 18.6 %all-to-all-start.5 = ((bf16[2,512,576]{1,2,0:T(8,128)(2,1)}), bf16[2,512,576]{1,2,0:T(8,128)(2,1)S(1)}, u32[]{:S(2)}, u32[]{:S(2)}) async-start(bf16[2,512,576]{1,2,0:T(8,128)(2,1)} %bitcast.21), calls=%async_computation.5 | async-start | bytes 2359296 | tf_op jit(solution)/shard_map/all_to_all | solution.py:38
  525.5 207.5 %all-to-all-start.6 = ((bf16[2,512,576]{1,2,0:T(8,128)(2,1)}), bf16[2,512,576]{1,2,0:T(8,128)(2,1)S(1)}, u32[]{:S(2)}, u32[]{:S(2)}) async-start(bf16[2,512,576]{1,2,0:T(8,128)(2,1)} %broadcast_in_dim.11), calls=%async_computation.6 | async-start | bytes 2359296 | tf_op jit(solution)/shard_map/all_to_all | solution.py:14
  730.7 7.4 copy-start.6
  733.0 264.8 %all-to-all-start.3 = ((bf16[2,512,512]{2,1,0:T(8,128)(2,1)}), bf16[2,512,512]{2,1,0:T(8,128)(2,1)}, u32[]{:S(2)}, u32[]{:S(2)}) async-start(bf16[2,512,512]{2,1,0:T(8,128)(2,1)} %bitcast.103), calls=%async_computation.3 | async-start | bytes 2097152 | tf_op jit(solution)/shard_map/all_to_all | solution.py:38
  852.5 130.7 %copy-start.5 = (bf16[512,1152]{0,1:T(8,128)(2,1)S(1)}, bf16[512,1152]{0,1:T(8,128)(2,1)}, u32[]{:S(2)}) copy-start(bf16[512,1152]{0,1:T(8,128)(2,1)} %fusion.35) | copy-start | bytes 3538948
  997.8 18.4 %all-to-all-start.7 = ((bf16[2,512,576]{1,2,0:T(8,128)(2,1)}), bf16[2,512,576]{1,2,0:T(8,128)(2,1)S(1)}, u32[]{:S(2)}, u32[]{:S(2)}) async-start(bf16[2,512,576]{1,2,0:T(8,128)(2,1)} %bitcast.28), calls=%async_computation.7 | async-start | bytes 2359296 | tf_op jit(solution)/shard_map/all_to_all | solution.py:38
Sparse Core Ops, SparseCore 0:
  11.8 114.9 all-gather.11
  130.6 100.1 all-gather.13
  234.4 115.1 all-gather.21
  353.1 119.4 all-gather.19
  476.0 116.5 all-gather.15
  596.1 116.5 all-gather.17
  716.3 127.0 all-gather.23
  847.0 127.0 all-gather.25
where the time goes:
time: 1030 us; the launch traced here: 1020 us
  waiting for transfers between devices  842 us (82%)
  local copies, waits for them, and re-layouts  71.3 us (7%)
  matrix products  46.9 us (5%)
  starting transfers between devices  30.7 us (3%)
  other arithmetic  18.8 us (2%)
  between operations  14.7 us (1%)
    all_gather x2, waiting for transfers between devices, encoder(): lax.all_gather(down_weight, 'dp', axis=1, tiled=True)  242 us
    all_gather x2, waiting for transfers between devices, encoder(): lax.all_gather(qkv_weight, 'dp', axis=0, tiled=True)  209 us
    all_gather x2, waiting for transfers between devices, encoder(): lax.all_gather(out_weight, 'dp', axis=1, tiled=True)  169 us
    all_gather x2, waiting for transfers between devices, encoder(): lax.all_gather(up_weight, 'dp', axis=0, tiled=True)  167 us
    all_to_all x4, waiting for transfers between devices, sum_at_owner(): lax.all_to_all(pieces, axis, split_axis=0, concat_axis=0, tiled=True)  38.1 us
    dot_general x2, matrix products, encoder(): jnp.dot(hidden, lax.all_gather(down_weight, 'dp', axis=1, tiled=True), pr...  30.1 us
    unnamed x29, local copies, waits for them, and re-layouts  28.5 us
  transfers between devices with their start and end apart: 16, of which 12 were waited for; matrix products, arithmetic and copies ran while one was open for 13% of the time, Pallas kernels for 0%

commit v1 on v0

--- a/solution.py
+++ b/solution.py
@@ -7,6 +7,11 @@
 HEADS = 16
 PATCHES = 256
 EPS = 1e-06
+
+
+def swapped_in(block, axis, dim):
+    outgoing = jnp.stack([block] * lax.axis_size(axis))
+    return jnp.concatenate(lax.all_to_all(outgoing, axis, 0, 0), axis=dim)
 
 
 def from_everyone(shard, axis):
@@ -82,9 +87,7 @@
     raised = fold_rows(second, lax.all_gather(up_weight, "dp", axis=0, tiled=True))
     hidden = jax.nn.gelu(raised, approximate=approx).astype(jnp.bfloat16)
     partial_mlp = jnp.dot(
-        hidden,
-        lax.all_gather(down_weight, "dp", axis=1, tiled=True),
-        preferred_element_type=jnp.float32,
+        hidden, swapped_in(down_weight, "dp", 1), preferred_element_type=jnp.float32
     )
     mlp_part = sum_at_owner(partial_mlp.astype(jnp.bfloat16), "mp", 1)
     return (middle.astype(jnp.float32) + mlp_part).astype(jnp.bfloat16)

time: 1030 us -> 965 us (0.937)
  waiting for transfers between devices: 842 us -> 719 us
  blocking collectives: 0 us -> 33.3 us
  starting transfers between devices: 30.7 us -> 48.5 us
    all_to_all x0 -> x2, waiting for transfers between devices: none -> 298 us  [swapped_in(): return jnp.concatenate(lax.all_to_all(outgoing, axis, 0, 0), axis=dim)]
    all_gather x2 -> x0, waiting for transfers between devices: 242 us -> none  [encoder(): lax.all_gather(down_weight, 'dp', axis=1, tiled=True)]
    all_gather x2, waiting for transfers between devices: 167 us -> 0.01 us  [encoder(): lax.all_gather(up_weight, 'dp', axis=0, tiled=True)]
    all_to_all x0 -> x2, blocking collectives: none -> 33.3 us  [the longest x1 17.3 us: sum_at_owner(): lax.all_to_all(pieces, axis, split_axis=0, concat_axis=0, tiled=True)]
    all_to_all x4 -> x3, waiting for transfers between devices: 38.1 us -> 11.2 us  [sum_at_owner(): lax.all_to_all(pieces, axis, split_axis=0, concat_axis=0, tiled=True)]
    all_to_all x0 -> x2, starting transfers between devices: none -> 26.1 us  [swapped_in(): return jnp.concatenate(lax.all_to_all(outgoing, axis, 0, 0), axis=dim)]
    all_gather x2, waiting for transfers between devices: 169 us -> 189 us  [encoder(): lax.all_gather(out_weight, 'dp', axis=1, tiled=True)]
    all_gather x2, waiting for transfers between devices: 209 us -> 196 us  [encoder(): lax.all_gather(qkv_weight, 'dp', axis=0, tiled=True)]
  transfers between devices with their start and end apart: 16 -> 14, of which waited for: 12 -> 9; matrix products, arithmetic and copies ran while one was open for 13% -> 14% of each run, Pallas kernels for 0% -> 0%
where the time goes in v1:
time: 965 us; the launch traced here: 953 us
  waiting for transfers between devices  719 us (75%)
  local copies, waits for them, and re-layouts  73.3 us (8%)
  starting transfers between devices  48.5 us (5%)
  matrix products  45.8 us (5%)
  blocking collectives  33.3 us (3%)
  other arithmetic  18.7 us (2%)
  between operations  14.7 us (2%)
    all_to_all x2, waiting for transfers between devices, swapped_in(): return jnp.concatenate(lax.all_to_all(outgoing, axis, 0, 0), axis=dim)  298 us
    all_gather x2, waiting for transfers between devices, encoder(): lax.all_gather(qkv_weight, 'dp', axis=0, tiled=True)  196 us
    all_gather x2, waiting for transfers between devices, encoder(): lax.all_gather(out_weight, 'dp', axis=1, tiled=True)  189 us
    dot_general x2, matrix products, encoder(): jnp.dot(hidden, swapped_in(down_weight, 'dp', 1), preferred_element_type=...  29 us
    all_to_all x2, starting transfers between devices, swapped_in(): return jnp.concatenate(lax.all_to_all(outgoing, axis, 0, 0), axis=dim)  26.1 us
    all_to_all x3, waiting for transfers between devices, from_everyone(): lax.all_to_all(jnp.broadcast_to(shard[None], (size, *shard.shape)), axis,...  21.3 us
    unnamed x38, local copies, waits for them, and re-layouts  20.4 us
  transfers between devices with their start and end apart: 14, of which 9 were waited for; matrix products, arithmetic and copies ran while one was open for 14% of the time, Pallas kernels for 0%

profile of v1, /device:TPU:1, one launch (start us, length us, event | category | flops | bytes accessed | tf_op | source)
XLA Modules:
  0.0 953.4 jit_solution(9698022035935879585)
XLA Ops:
  10.0 1.3 copy.45
  12.3 3.6 all-to-all-start
  16.0 11.5 %all-to-all-done = bf16[2,512,512]{1,2,0:T(8,128)(2,1)S(1)} async-done(((bf16[2,512,512]{1,2,0:T(8,128)(2,1)}), bf16[2,512,512]{1,2,0:T(8,128)(2,1)S(1)}, u32[]{:S(2)}, u32[]{:S(2)}) %all-to-all-start) | async-done | bytes 1048608 | tf_op jit(solution)/shard_map/all_to_all | solution.py:19
  28.6 3.6 all-to-all-start.5
  32.8 1.3 fusion.46
  34.1 9.7 %all-to-all-done.5 = bf16[2,512,576]{1,2,0:T(8,128)(2,1)S(1)} async-done(((bf16[2,512,576]{1,2,0:T(8,128)(2,1)}), bf16[2,512,576]{1,2,0:T(8,128)(2,1)S(1)}, u32[]{:S(2)}, u32[]{:S(2)}) %all-to-all-start.5) | async-done | bytes 1179680 | tf_op jit(solution)/shard_map/all_to_all | solution.py:19
  44.1 82.8 %all-gather.9.cloned.1.call-done = bf16[1024,3,512]{2,0,1:T(8,128)(2,1)} async-done(((bf16[8,3,512]{2,0,1:T(8,128)(2,1)}), bf16[1024,3,512]{2,0,1:T(8,128)(2,1)}) %all-gather.9.cloned.1.call-update) | async-done | bytes 3145744 | tf_op jit(solution)/shard_map/all_gather | solution.py:67
  126.8 4.7 copy.46
  131.5 4.1 convolution_convert_fusion.2
  135.6 3.2 reshape.190
  138.8 3.1 fusion.134
  141.8 2.5 copy.69
  144.3 1.4 copy.70
  146.3 2.0 fusion.94
  148.3 3.2 fusion.136
  152.7 78.2 %all-gather.11.cloned.1.call-done = bf16[512,1024]{0,1:T(8,128)(2,1)} async-done(((bf16[512,8]{0,1:T(8,128)(2,1)}), bf16[512,1024]{0,1:T(8,128)(2,1)}) %all-gather.11.cloned.1.call-update) | async-done | bytes 1048592 | tf_op jit(solution)/shard_map/all_gather | solution.py:80
  230.8 2.0 convolution_convert_fusion.4
  233.9 3.6 all-to-all-start.1
  237.8 1.4 fusion.34
  239.2 110.4 %all-gather.17.cloned.1.call-done = bf16[128,9,576]{2,1,0:T(8,128)(2,1)} async-done(((bf16[1,9,576]{2,1,0:T(8,128)(2,1)}), bf16[128,9,576]{2,1,0:T(8,128)(2,1)}) %all-gather.17.cloned.1.call-update) | async-done | bytes 1327120 | tf_op jit(solution)/shard_map/all_gather | solution.py:80
  349.6 4.1 reshape.187
  355.3 3.8 all-to-all-start.2
  359.1 113.5 %all-gather.15.cloned.1.call-done = bf16[1152,3,576]{2,1,0:T(4,128)(2,1)} async-done(((bf16[9,3,576]{2,1,0:T(4,128)(2,1)}), bf16[1152,3,576]{2,1,0:T(4,128)(2,1)}) %all-gather.15.cloned.1.call-update) | async-done | bytes 3981328 | tf_op jit(solution)/shard_map/all_gather | solution.py:67
  472.7 11.3 %copy.56 = bf16[1152,3,576]{0,2,1:T(8,128)(2,1)} copy(bf16[1152,3,576]{2,1,0:T(4,128)(2,1)} %all-gather.15.cloned.1.call-done) | data formatting | bytes 7962624 | tf_op jit(solution)/shard_map/all_gather | solution.py:67
  484.0 5.8 convolution_convert_fusion
  489.8 3.9 reshape.178
  493.7 1.2 fusion.135
  495.7 3.2 fusion.137
  500.4 1.3 convolution_convert_fusion.1
  502.3 17.3 %all_to_all.50 = bf16[2,512,576]{1,2,0:T(8,128)(2,1)S(1)} all-to-all(bf16[2,512,576]{1,2,0:T(8,128)(2,1)S(1)} %bitcast.109), channel_id=1, replica_groups=mesh['dp'=128,'mp'=2] {'mp'}, dimensions={0} | all-to-all | bytes 2359296 | tf_op jit(solution)/shard_map/all_to_all | solution.py:43
  519.5 2.5 stack.4
  522.0 10.4 %all-to-all-start.3 = ((bf16[128,2048,8]{1,2,0:T(8,128)(2,1)}), bf16[128,2048,8]{1,2,0:T(8,128)(2,1)}, u32[]{:S(2)}, u32[]{:S(2)}) async-start(bf16[128,2048,8]{1,2,0:T(8,128)(2,1)} %stack.4), calls=%async_computation.3 | async-start | bytes 8388608 | tf_op jit(solution)/shard_map/all_to_all | solution.py:14
  533.5 99.6 %all-to-all-done.3 = bf16[128,2048,8]{1,2,0:T(8,128)(2,1)} async-done(((bf16[128,2048,8]{1,2,0:T(8,128)(2,1)}), bf16[128,2048,8]{1,2,0:T(8,128)(2,1)}, u32[]{:S(2)}, u32[]{:S(2)}) %all-to-all-start.3) | async-done | bytes 4194336 | tf_op jit(solution)/shard_map/all_to_all | solution.py:14
  633.1 16.0 %all_to_all.51 = bf16[2,512,576]{1,2,0:T(8,128)(2,1)S(1)} all-to-all(bf16[2,512,576]{1,2,0:T(8,128)(2,1)S(1)} %broadcast_in_dim.11), channel_id=1, replica_groups=mesh['dp'=128,'mp'=2] {'mp'}, dimensions={0} | all-to-all | bytes 2359296 | tf_op jit(solution)/shard_map/all_to_all | solution.py:19
  649.1 4.1 stack.5
  653.2 15.7 %all-to-all-start.8 = ((bf16[128,2152,9]{1,2,0:T(8,128)(2,1)}), bf16[128,2152,9]{1,2,0:T(8,128)(2,1)}, u32[]{:S(2)}, u32[]{:S(2)}) async-start(bf16[128,2152,9]{1,2,0:T(8,128)(2,1)} %stack.5), calls=%async_computation.8 | async-start | bytes 17825792 | tf_op jit(solution)/shard_map/all_to_all | solution.py:14
  670.1 1.3 fusion.49
  671.4 16.9 %fusion.84 = bf16[512,1024]{1,0:T(8,128)(2,1)S(1)} fusion(bf16[128,2048,8]{1,2,0:T(8,128)(2,1)} %all-to-all-done.3, bf16[512,1024]{0,1:T(8,128)(2,1)} %fusion.49, bf16[1024,2048]{1,0:T(8,128)(2,1)} %all-gather.13.cloned.1.call-done), kind=kOutput, calls=%fused_computation.111 | convolution fusion | flops 4363649024 | bytes 10485760 | tf_op jit(solution)/shard_map/dot_general | solution.py:89
  690.0 1.4 fusion.37
  691.4 198.9 %all-to-all-done.8 = bf16[128,2152,9]{1,2,0:T(8,128)(2,1)} async-done(((bf16[128,2152,9]{1,2,0:T(8,128)(2,1)}), bf16[128,2152,9]{1,2,0:T(8,128)(2,1)}, u32[]{:S(2)}, u32[]{:S(2)}) %all-to-all-start.8) | async-done | bytes 4958240 | tf_op jit(solution)/shard_map/all_to_all | solution.py:14
  890.3 3.6 all-to-all-start.4
  893.9 9.1 reshape.182
  903.0 9.1 reshape.189
  912.2 12.1 %convolution_convert_fusion.3 = bf16[512,1152]{1,0:T(8,128)(2,1)} fusion(bf16[2152,1152]{0,1:T(8,128)(2,1)} %reshape.182, bf16[512,1152]{0,1:T(8,128)(2,1)S(1)} %copy-done.8, bf16[1152,2152]{1,0:T(8,128)(2,1)} %reshape.189), kind=kOutput, calls=%fused_computation.43 | convolution fusion | flops 5087711232 | bytes 12275712 | tf_op jit(solution)/shard_map/dot_general | solution.py:89
  924.3 2.5 copy.63
  927.8 3.6 all-to-all-start.9
  931.4 1.5 convert_reduce_fusion.4
  933.9 11.2 %all-to-all-done.9 = bf16[2,512,576]{1,2,0:T(8,128)(2,1)S(1)} async-done(((bf16[2,512,576]{1,2,0:T(8,128)(2,1)}), bf16[2,512,576]{1,2,0:T(8,128)(2,1)S(1)}, u32[]{:S(2)}, u32[]{:S(2)}) %all-to-all-start.9) | async-done | bytes 1179680 | tf_op jit(solution)/shard_map/all_to_all | solution.py:43
  (88 shorter events, 20.4 us)
Async XLA Ops:
  7.2 8.7 copy-start.12
  7.2 8.8 copy-start.14
  7.2 20.3 %copy-start.3 = (bf16[512,576]{0,1:T(8,128)(2,1)S(1)}, bf16[512,576]{0,1:T(8,128)(2,1)}, u32[]{:S(2)}) copy-start(bf16[512,576]{0,1:T(8,128)(2,1)} %param.15) | copy-start | bytes 1769476
  7.2 119.6 %all-gather.9.cloned.1.call-start = ((), (), s32[]{:S(2)}) async-start(), calls=%async_computation.10 | async-start | bytes 3170304 | tf_op jit(solution)/shard_map/all_gather | solution.py:67
  7.9 222.9 %all-gather.11.cloned.1.call-start = ((), (), s32[]{:S(2)}) async-start(), calls=%async_computation.11 | async-start | bytes 1056768 | tf_op jit(solution)/shard_map/all_gather | solution.py:80
  8.7 341.0 %all-gather.17.cloned.1.call-start = ((), (), s32[]{:S(2)}) async-start(), calls=%async_computation.14 | async-start | bytes 2641920 | tf_op jit(solution)/shard_map/all_gather | solution.py:80
  9.4 463.2 %all-gather.15.cloned.1.call-start = ((), (), s32[]{:S(2)}) async-start(), calls=%async_computation.13 | async-start | bytes 5944320 | tf_op jit(solution)/shard_map/all_gather | solution.py:67
  12.3 15.2 %all-to-all-start = ((bf16[2,512,512]{1,2,0:T(8,128)(2,1)}), bf16[2,512,512]{1,2,0:T(8,128)(2,1)S(1)}, u32[]{:S(2)}, u32[]{:S(2)}) async-start(bf16[2,512,512]{1,2,0:T(8,128)(2,1)} %broadcast_in_dim.8), calls=%async_computation | async-start | bytes 2097152 | tf_op jit(solution)/shard_map/all_to_all | solution.py:19
  28.6 15.2 %all-to-all-start.5 = ((bf16[2,512,576]{1,2,0:T(8,128)(2,1)}), bf16[2,512,576]{1,2,0:T(8,128)(2,1)S(1)}, u32[]{:S(2)}, u32[]{:S(2)}) async-start(bf16[2,512,576]{1,2,0:T(8,128)(2,1)} %broadcast_in_dim.10), calls=%async_computation.5 | async-start | bytes 2359296 | tf_op jit(solution)/shard_map/all_to_all | solution.py:19
  233.9 119.9 %all-to-all-start.1 = ((bf16[2,512,512]{2,1,0:T(8,128)(2,1)}), bf16[2,512,512]{2,1,0:T(8,128)(2,1)S(1)}, u32[]{:S(2)}, u32[]{:S(2)}) async-start(bf16[2,512,512]{2,1,0:T(8,128)(2,1)} %bitcast.108), calls=%async_computation.1 | async-start | bytes 2097152 | tf_op jit(solution)/shard_map/all_to_all | solution.py:43
  237.8 116.1 %copy-start.5 = (bf16[512,512]{1,0:T(8,128)(2,1)S(1)}, bf16[512,512]{1,0:T(8,128)(2,1)}, u32[]{:S(2)}) copy-start(bf16[512,512]{1,0:T(8,128)(2,1)} %param.14) | copy-start | bytes 1572868
  354.1 1.3 copy-start
  355.3 146.9 %all-to-all-start.2 = ((bf16[2,512,512]{1,2,0:T(8,128)(2,1)}), bf16[2,512,512]{1,2,0:T(8,128)(2,1)S(1)}, u32[]{:S(2)}, u32[]{:S(2)}) async-start(bf16[2,512,512]{1,2,0:T(8,128)(2,1)} %broadcast_in_dim.9), calls=%async_computation.2 | async-start | bytes 2097152 | tf_op jit(solution)/shard_map/all_to_all | solution.py:19
  359.1 124.9 %copy-start.7 = (bf16[2,512,576]{1,2,0:T(8,128)(2,1)S(1)}, bf16[2,512,576]{1,2,0:T(8,128)(2,1)}, u32[]{:S(2)}) copy-start(bf16[2,512,576]{1,2,0:T(8,128)(2,1)} %fusion.34) | copy-start | bytes 3538948
  499.0 1.4 copy-start.6
  500.4 19.2 %copy-start.10 = (bf16[2048,8]{0,1:T(8,128)(2,1)S(1)}, bf16[2048,8]{0,1:T(8,128)(2,1)}, u32[]{:S(2)}) copy-start(bf16[2048,8]{0,1:T(8,128)(2,1)} %param.21) | copy-start | bytes 98308
  522.0 11.2 %copy-start.4 = (bf16[512,576]{0,1:T(8,128)(2,1)S(1)}, bf16[512,576]{0,1:T(8,128)(2,1)}, u32[]{:S(2)}) copy-start(bf16[512,576]{0,1:T(8,128)(2,1)} %param.15) | copy-start | bytes 1769476
  522.0 111.0 %all-to-all-start.3 = ((bf16[128,2048,8]{1,2,0:T(8,128)(2,1)}), bf16[128,2048,8]{1,2,0:T(8,128)(2,1)}, u32[]{:S(2)}, u32[]{:S(2)}) async-start(bf16[128,2048,8]{1,2,0:T(8,128)(2,1)} %stack.4), calls=%async_computation.3 | async-start | bytes 8388608 | tf_op jit(solution)/shard_map/all_to_all | solution.py:14
  532.4 139.1 %all-gather.13.cloned.1.call-start = ((), (), s32[]{:S(2)}) async-start(), calls=%async_computation.12 | async-start | bytes 4227072 | tf_op jit(solution)/shard_map/all_gather | solution.py:87
  533.0 116.2 %copy-start.9 = (bf16[2152,9]{0,1:T(8,128)(2,1)S(1)}, bf16[2152,9]{0,1:T(8,128)(2,1)}, u32[]{:S(2)}) copy-start(bf16[2152,9]{0,1:T(8,128)(2,1)} %param.27) | copy-start | bytes 116212
  653.2 16.9 %copy-start.13 = (f32[1024]{0:T(1024)S(1)}, f32[1024]{0:T(1024)}, u32[]{:S(2)}) copy-start(f32[1024]{0:T(1024)} %param.19) | copy-start | bytes 12292
  653.2 237.1 %all-to-all-start.8 = ((bf16[128,2152,9]{1,2,0:T(8,128)(2,1)}), bf16[128,2152,9]{1,2,0:T(8,128)(2,1)}, u32[]{:S(2)}, u32[]{:S(2)}) async-start(bf16[128,2152,9]{1,2,0:T(8,128)(2,1)} %stack.5), calls=%async_computation.8 | async-start | bytes 17825792 | tf_op jit(solution)/shard_map/all_to_all | solution.py:14
  669.0 234.0 %all-gather.19.cloned.1.call-start = ((), (), s32[]{:S(2)}) async-start(), calls=%async_computation.15 | async-start | bytes 8982528 | tf_op jit(solution)/shard_map/all_gather | solution.py:87
  688.3 1.7 copy-start.11
  890.3 36.5 %all-to-all-start.4 = ((bf16[2,512,512]{2,1,0:T(8,128)(2,1)}), bf16[2,512,512]{2,1,0:T(8,128)(2,1)S(1)}, u32[]{:S(2)}, u32[]{:S(2)}) async-start(bf16[2,512,512]{2,1,0:T(8,128)(2,1)} %bitcast.106), calls=%async_computation.4 | async-start | bytes 2097152 | tf_op jit(solution)/shard_map/all_to_all | solution.py:43
  903.0 9.1 copy-start.8
  924.3 8.6 copy-start.1
  926.8 1.0 copy-start.2
  927.8 17.3 %all-to-all-start.9 = ((bf16[2,512,576]{1,2,0:T(8,128)(2,1)}), bf16[2,512,576]{1,2,0:T(8,128)(2,1)S(1)}, u32[]{:S(2)}, u32[]{:S(2)}) async-start(bf16[2,512,576]{1,2,0:T(8,128)(2,1)} %bitcast.29), calls=%async_computation.9 | async-start | bytes 2359296 | tf_op jit(solution)/shard_map/all_to_all | solution.py:43
Sparse Core Ops, SparseCore 0:
  11.8 114.9 all-gather.8
  130.6 100.2 all-gather.10
  234.4 115.1 all-gather.16
  353.2 119.4 all-gather.14
  536.5 130.3 all-gather.12
  673.1 181.9 all-gather.18
